TPU v7x, 32 devices: a whole 2x2x4 slice. The times are simulated.
32 devices in a mesh: row: 4 (over y, x), col: 8 (over z, core).
Axes of the slice: x: 2, y: 2, z: 4, core: 2. Of those that a mesh axis runs over, the one named last changes fastest.
Arguments:
- spectra: bfloat16 [16, 2048, 2048], P('row', None, 'col'), may hold values from -6 to 6
- coupling: float32 [16], replicated, may hold values from 0.2 to 1
Outputs:
- returned_spectra: bfloat16 [16, 2048, 2048], P('row', None, 'col')
All inputs are finite; a program needn't handle non-finite values.
Results may differ from a plain program's by a relative error of at most 0.0079.
Values may be sent and summed in bfloat16 or wider, within the bound.
No kernel may reach another device: no remote copies, remote signals or barrier semaphores. Data moves between devices by JAX's collectives and lax.ppermute only.
A program may use at most 128 MiB of HBM per device.

v0:
```python
import math
import jax
import jax.numpy as jnp
from jax import lax
from jax.sharding import PartitionSpec as P

NX = 3072
NY = 3072
M = 1024


def fourier_rows(mode_count, length, factor):
    wavenumber = jnp.arange(1, mode_count + 1, dtype=jnp.int32)
    position = jnp.arange(length, dtype=jnp.int32)
    residue = wavenumber[:, None] * position[None, :] % length
    angles = residue.astype(jnp.float32) * (2.0 * math.pi / length)
    table = jnp.concatenate([jnp.cos(angles), jnp.sin(angles)], 0) * factor
    return table.astype(jnp.bfloat16)


def ellipse(row_index, column_index, mode_count):
    row_waves = row_index % mode_count + 1
    col_waves = column_index % mode_count + 1
    inside = (
        row_waves[:, None] * row_waves[:, None] + col_waves[None, :] * col_waves[None, :]
        <= mode_count * mode_count
    )
    return inside.astype(jnp.float32)


def on_device(spectra, coupling):
    local_count = spectra.shape[0]
    width_here = spectra.shape[2]
    inverse_y = fourier_rows(M, NY, 1.0 / math.sqrt(M)).T
    inverse_x = fourier_rows(M, NX, 1.0 / math.sqrt(M))
    forward_x = fourier_rows(M, NX, 2.0 * math.sqrt(M) / NX).T
    forward_y = fourier_rows(M, NY, 2.0 * math.sqrt(M) / NY)
    half_done = jnp.einsum(
        "yk,fkc->fyc", inverse_y, spectra, preferred_element_type=jnp.float32
    ).astype(jnp.bfloat16)
    gathered = lax.all_to_all(half_done, "col", split_axis=1, concat_axis=2, tiled=True)
    first_field = lax.axis_index("row") * local_count
    strength = lax.dynamic_slice_in_dim(coupling, first_field, gathered.shape[0])
    gridded = jnp.einsum("fyk,kx->fyx", gathered, inverse_x, preferred_element_type=jnp.float32)
    tendency = (gridded + strength[:, None, None] * gridded * gridded).astype(jnp.bfloat16)
    projected = jnp.einsum(
        "fyx,xk->fyk", tendency, forward_x, preferred_element_type=jnp.float32
    ).astype(jnp.bfloat16)
    returned = lax.all_to_all(projected, "col", split_axis=2, concat_axis=1, tiled=True)
    result = jnp.einsum("ky,fyc->fkc", forward_y, returned, preferred_element_type=jnp.float32)
    columns = lax.axis_index("col") * width_here + jnp.arange(width_here, dtype=jnp.int32)
    inside = ellipse(jnp.arange(2 * M, dtype=jnp.int32), columns, M)
    return (result * inside[None, :, :]).astype(jnp.bfloat16)


def solution(mesh):
    placed = (P("row", None, "col"), P())
    return jax.shard_map(
        on_device, mesh=mesh, in_specs=placed, out_specs=P("row", None, "col"), check_vma=False
    )
```

profile of v0, /device:TPU:0, one launch (start us, length us, event | category | flops | bytes accessed | tf_op | source)
XLA Modules:
  0.0 505.0 jit_solution(3590374729908584467)
XLA Ops:
  0.0 52.6 %fusion.8 = (f32[1024,3072]{0,1:T(8,128)}, f32[1024,3072]{0,1:T(8,128)}) fusion(s32[1024]{0:T(1024)S(1)} %iota_add_fusion), kind=kLoop, calls=%fused_computation.14 | loop fusion | flops 28311552 | bytes 25169920 | tf_op jit(solution)/shard_map/cos | solution.py:17
  52.6 20.9 %convert_bitcast_fusion = bf16[4,3072,256]{2,1,0:T(8,128)(2,1)} fusion(bf16[4,2048,256]{2,1,0:T(8,128)(2,1)} %param.2, f32[1024,3072]{0,1:T(8,128)} %get-tuple-element.6, f32[1024,3072]{0,1:T(8,128)} %get-tuple-element.5), kind=kOutput, calls=%fused_computation.23 | convolution fusion | flops 12906921984 | bytes 35651584 | tf_op jit(solution)/shard_map/yk,fkc->fyc/dot_general | solution.py:38
  73.5 0.0 copy-start
  73.5 10.5 %copy.9 = bf16[4,3072,256]{2,0,1:T(4,128)(2,1)} copy(bf16[4,3072,256]{2,1,0:T(8,128)(2,1)} %convert_bitcast_fusion) | data formatting | bytes 12582912 | tf_op jit(solution)/shard_map/convert_element_type | solution.py:40
  84.0 6.4 %all-to-all-start = ((bf16[4,3072,256]{2,0,1:T(4,128)(2,1)}), bf16[4,3072,256]{2,0,1:T(4,128)(2,1)}, u32[]{:S(2)}, u32[]{:S(2)}) async-start(bf16[4,3072,256]{2,0,1:T(4,128)(2,1)} %copy.9), calls=%async_computation | async-start | bytes 12582912 | tf_op jit(solution)/shard_map/all_to_all | solution.py:41
  90.4 0.0 copy-done
  90.4 0.1 dynamic_slice.3
  90.5 138.9 %all-to-all-done = bf16[4,3072,256]{2,0,1:T(4,128)(2,1)} async-done(((bf16[4,3072,256]{2,0,1:T(4,128)(2,1)}), bf16[4,3072,256]{2,0,1:T(4,128)(2,1)}, u32[]{:S(2)}, u32[]{:S(2)}) %all-to-all-start) | async-done | bytes 6291488 | tf_op jit(solution)/shard_map/all_to_all | solution.py:41
  229.4 9.1 %copy.26 = bf16[4,8,384,256]{3,1,2,0:T(8,128)(2,1)} copy(bf16[4,8,384,256]{3,0,2,1:T(4,128)(2,1)} %bitcast.2) | data formatting | bytes 12582912 | tf_op jit(solution)/shard_map/all_to_all | solution.py:41
  238.5 10.4 %all_to_all.29 = bf16[4,384,2048]{2,1,0:T(8,128)(2,1)} reshape(bf16[4,384,8,256]{3,2,1,0:T(8,128)(2,1)} %bitcast.46) | data formatting | bytes 12582912 | tf_op jit(solution)/shard_map/all_to_all | solution.py:41
  248.9 27.8 %fusion.59 = bf16[4,384,3072]{2,1,0:T(8,128)(2,1)} fusion(bf16[4,384,2048]{2,1,0:T(8,128)(2,1)} %all_to_all.29, f32[4]{0:T(128)S(1)} %dynamic_slice.3, f32[1024,3072]{0,1:T(8,128)} %get-tuple-element.6, f32[1024,3072]{0,1:T(8,128)} %get-tuple-element.5), kind=kOutput, calls=%fused_computation.5.clone.clone.clone.clone.2 | convolution fusion | flops 19365101568 | bytes 40894480 | tf_op jit(solution)/shard_map/fyk,kx->fyx/dot_general | solution.py:44
  276.7 27.5 %fusion.16 = bf16[4,384,2048]{2,1,0:T(8,128)(2,1)} fusion(f32[1024,3072]{0,1:T(8,128)} %get-tuple-element.6, f32[1024,3072]{0,1:T(8,128)} %get-tuple-element.5, bf16[4,384,3072]{2,1,0:T(8,128)(2,1)} %fusion.59), kind=kOutput, calls=%fused_computation.24 | convolution fusion | flops 19349372928 | bytes 40894464 | tf_op jit(solution)/shard_map/fyx,xk->fyk/dot_general | solution.py:46
  304.2 10.7 %copy.13 = bf16[4,384,2048]{1,0,2:T(4,128)(2,1)} copy(bf16[4,384,2048]{2,1,0:T(8,128)(2,1)} %fusion.16) | data formatting | bytes 12582912 | tf_op jit(solution)/shard_map/convert_element_type | solution.py:48
  315.0 4.8 all-to-all-start.1
  319.8 0.3 fusion.19
  320.1 138.6 %all-to-all-done.1 = bf16[4,384,2048]{1,0,2:T(4,128)(2,1)} async-done(((bf16[4,384,2048]{1,0,2:T(4,128)(2,1)}), bf16[4,384,2048]{1,0,2:T(4,128)(2,1)}, u32[]{:S(2)}, u32[]{:S(2)}) %all-to-all-start.1) | async-done | bytes 6291488 | tf_op jit(solution)/shard_map/all_to_all | solution.py:49
  458.7 9.2 %copy.25 = bf16[4,384,8,256]{1,2,3,0:T(8,128)(2,1)} copy(bf16[4,384,8,256]{1,0,3,2:T(4,128)(2,1)} %bitcast.6) | data formatting | bytes 12582912 | tf_op jit(solution)/shard_map/all_to_all | solution.py:49
  467.9 10.4 %all_to_all.33 = bf16[4,3072,256]{1,2,0:T(8,128)(2,1)} reshape(bf16[4,8,384,256]{2,1,3,0:T(8,128)(2,1)} %bitcast.47) | data formatting | bytes 12582912 | tf_op jit(solution)/shard_map/all_to_all | solution.py:49
  478.3 20.5 %fusion.15 = bf16[4,2048,256]{1,2,0:T(8,128)(2,1)} fusion(bf16[4,3072,256]{1,2,0:T(8,128)(2,1)} %all_to_all.33, f32[2048,256]{0,1:T(8,128)S(1)} %fusion.19, f32[1024,3072]{0,1:T(8,128)} %get-tuple-element.6, f32[1024,3072]{0,1:T(8,128)} %get-tuple-element.5), kind=kOutput, calls=%fused_computation.20 | convolution fusion | flops 12907970560 | bytes 37748736 | tf_op jit(solution)/shard_map/ky,fyc->fkc/dot_general | solution.py:50
  498.8 6.2 %copy.16 = bf16[4,2048,256]{2,1,0:T(8,128)(2,1)} copy(bf16[4,2048,256]{1,2,0:T(8,128)(2,1)} %fusion.15) | data formatting | bytes 8388608 | tf_op jit(solution)/shard_map/convert_element_type | solution.py:53
  (3 shorter events, 0.0 us)
Async XLA Ops:
  73.5 16.9 %copy-start = (f32[16]{0:T(128)S(1)}, f32[16]{0:T(128)}, u32[]{:S(2)}) copy-start(f32[16]{0:T(128)} %param.3) | copy-start | bytes 196
  84.0 145.4 %all-to-all-start = ((bf16[4,3072,256]{2,0,1:T(4,128)(2,1)}), bf16[4,3072,256]{2,0,1:T(4,128)(2,1)}, u32[]{:S(2)}, u32[]{:S(2)}) async-start(bf16[4,3072,256]{2,0,1:T(4,128)(2,1)} %copy.9), calls=%async_computation | async-start | bytes 12582912 | tf_op jit(solution)/shard_map/all_to_all | solution.py:41
  315.0 143.7 %all-to-all-start.1 = ((bf16[4,384,2048]{1,0,2:T(4,128)(2,1)}), bf16[4,384,2048]{1,0,2:T(4,128)(2,1)}, u32[]{:S(2)}, u32[]{:S(2)}) async-start(bf16[4,384,2048]{1,0,2:T(4,128)(2,1)} %copy.13), calls=%async_computation.1 | async-start | bytes 12582912 | tf_op jit(solution)/shard_map/all_to_all | solution.py:49
where the time goes:
time: 506 us; the launch traced here: 505 us
  waiting for transfers between devices  278 us (55%)
  matrix products  96.8 us (19%)
  local copies, waits for them, and re-layouts  66.6 us (13%)
  other arithmetic  52.9 us (10%)
  starting transfers between devices  11.1 us (2%)
    all_to_all x1, waiting for transfers between devices, on_device(): lax.all_to_all(half_done, 'col', split_axis=1, concat_axis=2, tiled=True)  139 us
    all_to_all x1, waiting for transfers between devices, on_device(): lax.all_to_all(projected, 'col', split_axis=2, concat_axis=1, tiled=True)  139 us
    cos x1, other arithmetic, fourier_rows(): table = jnp.concatenate([jnp.cos(angles), jnp.sin(angles)], 0) * factor  52.6 us
    dot_general x1, matrix products, on_device(): jnp.einsum('fyk,kx->fyx', gathered, inverse_x, preferred_element_type=jnp...  27.8 us
    dot_general x1, matrix products, on_device(): jnp.einsum('fyx,xk->fyk', tendency, forward_x, preferred_element_type=jnp...  27.5 us
    dot_general x1, matrix products, on_device(): jnp.einsum('yk,fkc->fyc', inverse_y, spectra, preferred_element_type=jnp....  20.9 us
    dot_general x1, matrix products, on_device(): jnp.einsum('ky,fyc->fkc', forward_y, returned, preferred_element_type=jnp...  20.5 us
    all_to_all x2, local copies, waits for them, and re-layouts, on_device(): lax.all_to_all(projected, 'col', split_axis=2, concat_axis=1, tiled=True)  19.6 us
  transfers between devices with their start and end apart: 2, of which 2 were waited for; matrix products, arithmetic and copies ran while one was open for 0% of the time, Pallas kernels for 0%

commit v1 on v0

--- a/solution.py
+++ b/solution.py
@@ -46,7 +46,9 @@
     projected = jnp.einsum(
         "fyx,xk->fyk", tendency, forward_x, preferred_element_type=jnp.float32
     ).astype(jnp.bfloat16)
-    returned = lax.all_to_all(projected, "col", split_axis=2, concat_axis=1, tiled=True)
+    parts = jnp.split(projected, lax.axis_size("col"), axis=2)
+    incoming = lax.all_to_all(jnp.stack(parts), "col", 0, 0)
+    returned = jnp.concatenate(incoming, axis=1)
     result = jnp.einsum("ky,fyc->fkc", forward_y, returned, preferred_element_type=jnp.float32)
     columns = lax.axis_index("col") * width_here + jnp.arange(width_here, dtype=jnp.int32)
     inside = ellipse(jnp.arange(2 * M, dtype=jnp.int32), columns, M)

time: 506 us -> 487 us (0.962)
  local copies, waits for them, and re-layouts: 66.6 us -> 50.5 us
    all_to_all x2 -> x0, local copies, waits for them, and re-layouts: 19.6 us -> none  [on_device(): lax.all_to_all(projected, 'col', split_axis=2, concat_axis=1, tiled=True)]
    convert_element_type x1 -> x0, local copies, waits for them, and re-layouts: 10.7 us -> none  [on_device(): projected = jnp.einsum('fyx,xk->fyk', tendency, forward_x, preferred_elem...]
    unnamed x2 -> x9, local copies, waits for them, and re-layouts: 0.01 us -> 7.06 us
    reshape x0 -> x1, local copies, waits for them, and re-layouts: none -> 6.14 us  [on_device(): returned = jnp.concatenate(incoming, axis=1)]
where the time goes in v1:
time: 487 us; the launch traced here: 486 us
  waiting for transfers between devices  277 us (57%)
  matrix products  94.1 us (19%)
  other arithmetic  52.9 us (11%)
  local copies, waits for them, and re-layouts  50.5 us (10%)
  starting transfers between devices  11.5 us (2%)
    all_to_all x1, waiting for transfers between devices, on_device(): lax.all_to_all(half_done, 'col', split_axis=1, concat_axis=2, tiled=True)  139 us
    all_to_all x1, waiting for transfers between devices, on_device(): incoming = lax.all_to_all(jnp.stack(parts), 'col', 0, 0)  138 us
    cos x1, other arithmetic, fourier_rows(): table = jnp.concatenate([jnp.cos(angles), jnp.sin(angles)], 0) * factor  52.6 us
    dot_general x1, matrix products, on_device(): jnp.einsum('fyk,kx->fyx', gathered, inverse_x, preferred_element_type=jnp...  27.8 us
    dot_general x1, matrix products, on_device(): jnp.einsum('fyx,xk->fyk', tendency, forward_x, preferred_element_type=jnp...  24.9 us
    dot_general x1, matrix products, on_device(): jnp.einsum('yk,fkc->fyc', inverse_y, spectra, preferred_element_type=jnp....  20.9 us
    dot_general x1, matrix products, on_device(): jnp.einsum('ky,fyc->fkc', forward_y, returned, preferred_element_type=jnp...  20.5 us
    all_to_all x2, local copies, waits for them, and re-layouts, on_device(): lax.all_to_all(half_done, 'col', split_axis=1, concat_axis=2, tiled=True)  19.5 us
  transfers between devices with their start and end apart: 2, of which 2 were waited for; matrix products, arithmetic and copies ran while one was open for 0% of the time, Pallas kernels for 0%

profile of v1, /device:TPU:0, one launch (start us, length us, event | category | flops | bytes accessed | tf_op | source)
XLA Modules:
  0.0 486.3 jit_solution(2253539418045676433)
XLA Ops:
  0.0 52.6 %fusion.8 = (f32[1024,3072]{0,1:T(8,128)}, f32[1024,3072]{0,1:T(8,128)}) fusion(s32[1024]{0:T(1024)S(1)} %iota_add_fusion), kind=kLoop, calls=%fused_computation.14 | loop fusion | flops 28311552 | bytes 25169920 | tf_op jit(solution)/shard_map/cos | solution.py:17
  52.6 20.9 %convert_bitcast_fusion = bf16[4,3072,256]{2,1,0:T(8,128)(2,1)} fusion(bf16[4,2048,256]{2,1,0:T(8,128)(2,1)} %param.2, f32[1024,3072]{0,1:T(8,128)} %get-tuple-element.6, f32[1024,3072]{0,1:T(8,128)} %get-tuple-element.5), kind=kOutput, calls=%fused_computation.22 | convolution fusion | flops 12906921984 | bytes 35651584 | tf_op jit(solution)/shard_map/yk,fkc->fyc/dot_general | solution.py:38
  73.5 10.5 %copy.15 = bf16[4,3072,256]{2,0,1:T(4,128)(2,1)} copy(bf16[4,3072,256]{2,1,0:T(8,128)(2,1)} %convert_bitcast_fusion) | data formatting | bytes 12582912 | tf_op jit(solution)/shard_map/convert_element_type | solution.py:40
  84.0 0.0 copy-start
  84.0 6.5 %all-to-all-start = ((bf16[4,3072,256]{2,0,1:T(4,128)(2,1)}), bf16[4,3072,256]{2,0,1:T(4,128)(2,1)}, u32[]{:S(2)}, u32[]{:S(2)}) async-start(bf16[4,3072,256]{2,0,1:T(4,128)(2,1)} %copy.15), calls=%async_computation | async-start | bytes 12582912 | tf_op jit(solution)/shard_map/all_to_all | solution.py:41
  90.5 0.0 copy-done
  90.5 0.1 dynamic_slice.3
  90.6 138.9 %all-to-all-done = bf16[4,3072,256]{2,0,1:T(4,128)(2,1)} async-done(((bf16[4,3072,256]{2,0,1:T(4,128)(2,1)}), bf16[4,3072,256]{2,0,1:T(4,128)(2,1)}, u32[]{:S(2)}, u32[]{:S(2)}) %all-to-all-start) | async-done | bytes 6291488 | tf_op jit(solution)/shard_map/all_to_all | solution.py:41
  229.5 9.1 %copy.31 = bf16[4,8,384,256]{3,1,2,0:T(8,128)(2,1)} copy(bf16[4,8,384,256]{3,0,2,1:T(4,128)(2,1)} %bitcast.2) | data formatting | bytes 12582912 | tf_op jit(solution)/shard_map/all_to_all | solution.py:41
  238.6 10.4 %all_to_all.19 = bf16[4,384,2048]{2,1,0:T(8,128)(2,1)} reshape(bf16[4,384,8,256]{3,2,1,0:T(8,128)(2,1)} %bitcast.72) | data formatting | bytes 12582912 | tf_op jit(solution)/shard_map/all_to_all | solution.py:41
  249.0 27.8 %fusion.67 = bf16[4,384,3072]{2,1,0:T(8,128)(2,1)} fusion(bf16[4,384,2048]{2,1,0:T(8,128)(2,1)} %all_to_all.19, f32[4]{0:T(128)S(1)} %dynamic_slice.3, f32[1024,3072]{0,1:T(8,128)} %get-tuple-element.6, f32[1024,3072]{0,1:T(8,128)} %get-tuple-element.5), kind=kOutput, calls=%fused_computation.5.clone.clone.clone.clone.2 | convolution fusion | flops 19365101568 | bytes 40894480 | tf_op jit(solution)/shard_map/fyk,kx->fyx/dot_general | solution.py:44
  276.8 24.9 %fusion.16 = bf16[4,384,2048]{2,1,0:T(8,128)(2,1)S(1)} fusion(f32[1024,3072]{0,1:T(8,128)} %get-tuple-element.6, f32[1024,3072]{0,1:T(8,128)} %get-tuple-element.5, bf16[4,384,3072]{2,1,0:T(8,128)(2,1)} %fusion.67), kind=kOutput, calls=%fused_computation.23 | convolution fusion | flops 19349372928 | bytes 40894464 | tf_op jit(solution)/shard_map/fyx,xk->fyk/dot_general | solution.py:46
  301.7 1.0 fusion.32
  302.7 1.0 fusion.31
  303.7 1.0 fusion.30
  304.7 1.0 fusion.29
  305.7 1.0 fusion.28
  306.7 1.0 fusion.27
  307.7 1.0 fusion.26
  308.8 1.0 fusion.25
  309.8 5.0 %all-to-all-start.1 = ((bf16[8,4,384,256]{3,2,1,0:T(8,128)(2,1)}), bf16[8,4,384,256]{3,2,1,0:T(8,128)(2,1)}, u32[]{:S(2)}, u32[]{:S(2)}) async-start(bf16[8,4,384,256]{3,2,1,0:T(8,128)(2,1)} %fusion.25), calls=%async_computation.1 | async-start | bytes 12582912 | tf_op jit(solution)/shard_map/all_to_all | solution.py:50
  314.8 0.3 fusion.19
  315.1 138.3 %all-to-all-done.1 = bf16[8,4,384,256]{3,2,1,0:T(8,128)(2,1)} async-done(((bf16[8,4,384,256]{3,2,1,0:T(8,128)(2,1)}), bf16[8,4,384,256]{3,2,1,0:T(8,128)(2,1)}, u32[]{:S(2)}, u32[]{:S(2)}) %all-to-all-start.1) | async-done | bytes 6291488 | tf_op jit(solution)/shard_map/all_to_all | solution.py:50
  453.4 6.1 %copy.19 = bf16[4,8,384,256]{3,2,1,0:T(8,128)(2,1)} copy(bf16[4,8,384,256]{3,2,0,1:T(8,128)(2,1)} %bitcast.14) | data formatting | bytes 12582912 | tf_op jit(solution)/shard_map/reshape | solution.py:51
  459.6 20.5 %fusion.15 = bf16[4,2048,256]{1,2,0:T(8,128)(2,1)} fusion(bf16[4,3072,256]{2,1,0:T(8,128)(2,1)} %bitcast.73, f32[2048,256]{0,1:T(8,128)S(1)} %fusion.19, f32[1024,3072]{0,1:T(8,128)} %get-tuple-element.6, f32[1024,3072]{0,1:T(8,128)} %get-tuple-element.5), kind=kOutput, calls=%fused_computation.20 | convolution fusion | flops 12907970560 | bytes 37748736 | tf_op jit(solution)/shard_map/ky,fyc->fkc/dot_general | solution.py:52
  480.1 6.2 %copy.22 = bf16[4,2048,256]{2,1,0:T(8,128)(2,1)} copy(bf16[4,2048,256]{1,2,0:T(8,128)(2,1)} %fusion.15) | data formatting | bytes 8388608 | tf_op jit(solution)/shard_map/convert_element_type | solution.py:55
  (3 shorter events, 0.0 us)
Async XLA Ops:
  84.0 6.5 %copy-start = (f32[16]{0:T(128)S(1)}, f32[16]{0:T(128)}, u32[]{:S(2)}) copy-start(f32[16]{0:T(128)} %param.3) | copy-start | bytes 196
  84.0 145.5 %all-to-all-start = ((bf16[4,3072,256]{2,0,1:T(4,128)(2,1)}), bf16[4,3072,256]{2,0,1:T(4,128)(2,1)}, u32[]{:S(2)}, u32[]{:S(2)}) async-start(bf16[4,3072,256]{2,0,1:T(4,128)(2,1)} %copy.15), calls=%async_computation | async-start | bytes 12582912 | tf_op jit(solution)/shard_map/all_to_all | solution.py:41
  309.8 143.7 %all-to-all-start.1 = ((bf16[8,4,384,256]{3,2,1,0:T(8,128)(2,1)}), bf16[8,4,384,256]{3,2,1,0:T(8,128)(2,1)}, u32[]{:S(2)}, u32[]{:S(2)}) async-start(bf16[8,4,384,256]{3,2,1,0:T(8,128)(2,1)} %fusion.25), calls=%async_computation.1 | async-start | bytes 12582912 | tf_op jit(solution)/shard_map/all_to_all | solution.py:50
